TPU v7x, 32 devices: a whole 2x2x4 slice. The times are simulated.
32 devices in a mesh: grid: 8 (over y, x, core), rows: 4 (over z).
Axes of the slice: x: 2, y: 2, z: 4, core: 2. Of those that a mesh axis runs over, the one named last changes fastest.
Arguments:
- density: bfloat16 [32, 128, 4096], P(None, 'rows', 'grid'), as said below
- basis_values: bfloat16 [16, 16, 128, 512], P('grid', None, 'rows'), may hold values from -0.59765625 to 0.59765625
- grid_points: float32 [16, 3, 512], P('grid'), may hold values from -4 to 4
- grid_weights: float32 [16, 512], P('grid'), may hold values from 0.05 to 1
- screened_blocks: int32 [16, 16], P('grid'), may hold values from 0 to 31, as said below
Outputs:
- exchange: float32 [32, 128, 4096], P(None, 'rows', 'grid')
Inputs may be any that keep to these rules, and one draw needn't show every extreme that they name: density is symmetric: density[a, i, b * 128 + j] equals density[b, j, a * 128 + i]. `screened_blocks`: each row holds 16 distinct block numbers.
All inputs are finite; a program needn't handle non-finite values.
Results may differ from a plain program's by a relative error of at most 0.00055.
The roundings to bfloat16 on the way count: a program that leaves them out, or rounds other values in their place, can miss the bound.
Values may be sent and summed in bfloat16 or wider, within the bound.
A program may use at most 128 MiB of HBM per device.

v0:
```python
import jax
import jax.numpy as jnp
from jax import lax
from jax.sharding import PartitionSpec as P


def body(density, basis_values, grid_points, grid_weights, screened_blocks):
    nblocks = density.shape[0]
    rows_mine = density.shape[1]
    block_size = rows_mine * lax.axis_size("rows")
    nbasis = nblocks * block_size
    nsig = basis_values.shape[1]
    npoints = basis_values.shape[3]
    stripe = lax.all_gather(density, "grid", axis=2, tiled=True)
    totals = jnp.zeros((nblocks, rows_mine, nblocks, block_size), jnp.float32)
    for batch_index in range(basis_values.shape[0]):
        blocks = screened_blocks[batch_index]
        row_pick = jnp.take(stripe, blocks, axis=0).reshape(nsig * rows_mine, nblocks, block_size)
        chosen = jnp.take(row_pick, blocks, axis=1)
        local_values = basis_values[batch_index]
        x_mine = local_values.reshape(nsig * rows_mine, npoints)
        fsum = jnp.einsum(
            "mtk,tkp->mp",
            chosen,
            lax.all_gather(local_values, "rows", axis=1, tiled=True),
            preferred_element_type=jnp.float32,
        )
        fmat = fsum.astype(jnp.bfloat16)
        intersection_part = lax.dot_general(
            x_mine, fmat, (((0,), (0,)), ((), ())), preferred_element_type=jnp.float32
        )
        intersection = lax.psum(intersection_part, "rows")
        places = grid_points[batch_index]
        weights = grid_weights[batch_index]
        diffs = places[:, :, None] - places[:, None, :]
        kern = 1.0 / jnp.sqrt(jnp.sum(diffs * diffs, axis=0) + 0.5)
        mixed = (weights[:, None] * kern * intersection).astype(jnp.bfloat16)
        potential = (
            jnp.dot(x_mine, mixed, preferred_element_type=jnp.float32) * weights[None, :]
        ).astype(jnp.bfloat16)
        potential = potential.reshape(nsig, rows_mine, npoints)
        block_k = jnp.einsum(
            "mp,tkp->mtk",
            x_mine,
            lax.all_gather(potential, "rows", axis=1, tiled=True),
            preferred_element_type=jnp.float32,
        )
        block_k = block_k.reshape(nsig, rows_mine, nsig, block_size)
        totals = totals.at[blocks[:, None], :, blocks[None, :], :].add(
            block_k.transpose(0, 2, 1, 3)
        )
    return lax.psum_scatter(
        totals.reshape(nblocks, rows_mine, nbasis), "grid", scatter_dimension=2, tiled=True
    )


def solution(mesh):
    placed = (
        P(None, "rows", "grid"),
        P("grid", None, "rows", None),
        P("grid", None, None),
        P("grid", None),
        P("grid", None),
    )
    return jax.shard_map(
        body, mesh=mesh, in_specs=placed, out_specs=P(None, "rows", "grid"), check_vma=False
    )
```

profile of v0, /device:TPU:0, one launch (start us, length us, event | category | flops | bytes accessed | tf_op | source)
XLA Modules:
  0.0 572.5 jit_solution(16403228100501752769)
XLA Ops:
  6.5 0.7 all-gather.8.cloned.1.call-update
  7.3 0.0 all-gather.16.cloned.1.call-start
  7.3 2.3 fusion.56
  9.6 0.0 all-gather.14.cloned.1.call-start
  9.7 0.7 all-gather.14.cloned.1.call-update
  10.4 0.0 all-reduce.3.cloned.1.call-start
  10.5 57.3 %all-gather.8.cloned.1.call-done = bf16[32,32,4096]{2,1,0:T(8,128)(2,1)} async-done(((bf16[32,32,512]{2,1,0:T(8,128)(2,1)}), bf16[32,32,4096]{2,1,0:T(8,128)(2,1)}) %all-gather.8.cloned.1.call-update) | async-done | bytes 8388624 | tf_op jit(solution)/shard_map/all_gather | solution.py:14
  67.8 6.2 %gather_fusion.2 = bf16[16,32,4096]{2,1,0:T(8,128)(2,1)} fusion(bf16[32,32,4096]{2,1,0:T(8,128)(2,1)} %all-gather.8.cloned.1.call-done, s32[1024]{0:T(1024)S(1)} %pad_clamp_fusion), kind=kCustom, calls=%fused_computation.2.clone | custom fusion | bytes 8388672 | tf_op jit(solution)/shard_map/jit(_take)/gather | solution.py:18
  74.0 2.7 broadcast_select_fusion
  76.7 1.3 copy.31
  78.0 3.6 copy.23
  81.6 3.1 gather_fusion.3
  84.8 6.2 %gather_fusion = bf16[16,32,4096]{2,1,0:T(8,128)(2,1)} fusion(bf16[32,32,4096]{2,1,0:T(8,128)(2,1)} %all-gather.8.cloned.1.call-done, s32[1024]{0:T(1024)S(1)} %pad_clamp_fusion.1), kind=kCustom, calls=%fused_computation.clone | custom fusion | bytes 8388672 | tf_op jit(solution)/shard_map/jit(_take)/gather | solution.py:18
  91.0 2.7 broadcast_select_fusion.1
  93.6 1.3 copy.30
  94.9 3.6 copy.19
  98.5 4.4 gather_fusion.1
  102.9 12.2 %all-gather.16.cloned.1.call-done = bf16[1,16,128,512]{3,2,1,0:T(8,128)(2,1)} async-done(((bf16[1,16,32,512]{3,2,1,0:T(8,128)(2,1)}), bf16[1,16,128,512]{3,2,1,0:T(8,128)(2,1)}) %all-gather.16.cloned.1.call-update) | async-done | bytes 2097168 | tf_op jit(solution)/shard_map/all_gather | solution.py:25
  115.1 4.3 convolution_bitcast_fusion.2
  119.4 41.8 %all-gather.14.cloned.1.call-done = bf16[1,16,128,512]{3,2,1,0:T(8,128)(2,1)} async-done(((bf16[1,16,32,512]{3,2,1,0:T(8,128)(2,1)}), bf16[1,16,128,512]{3,2,1,0:T(8,128)(2,1)}) %all-gather.14.cloned.1.call-update) | async-done | bytes 2097168 | tf_op jit(solution)/shard_map/all_gather | solution.py:25
  161.2 4.9 convolution_bitcast_fusion.3
  166.0 0.0 all-reduce.3.cloned.1.call-update
  166.1 0.0 all-gather.10.cloned.1.call-start
  166.2 0.4 multiply_reduce_fusion.1
  166.5 0.3 copy.18
  166.9 84.3 %all-reduce.3.cloned.1.call-done = (f32[512,512]{0,1:T(8,128)}, f32[512,512]{0,1:T(8,128)}) async-done(((f32[512,512]{0,1:T(8,128)}, f32[512,512]{0,1:T(8,128)}), (f32[512,512]{0,1:T(8,128)}, f32[512,512]{0,1:T(8,128)})) %all-reduce.3.cloned.1.call-update) | async-done | bytes 2097168 | tf_op jit(solution)/shard_map/psum | solution.py:32
  251.2 2.5 fusion.20
  253.7 0.0 all-gather.12.cloned.1.call-start
  253.8 0.4 multiply_reduce_fusion
  254.2 0.3 copy.22
  254.5 2.5 fusion.21
  257.0 0.2 reduce-scatter.2.cloned.1.call-start
  257.3 0.1 or_select_fusion
  257.4 0.1 reshape.132
  257.5 0.1 reshape.138
  257.6 41.0 %all-gather.10.cloned.1.call-done = bf16[16,128,512]{2,1,0:T(8,128)(2,1)} async-done(((bf16[16,32,512]{2,1,0:T(8,128)(2,1)}), bf16[16,128,512]{2,1,0:T(8,128)(2,1)}) %all-gather.10.cloned.1.call-update) | async-done | bytes 2097168 | tf_op jit(solution)/shard_map/all_gather | solution.py:45
  298.6 4.8 convolution_bitcast_fusion.1
  303.4 5.5 copy.20
  309.0 5.5 copy.21
  314.4 30.1 %all-gather.12.cloned.1.call-done = bf16[16,128,512]{2,1,0:T(8,128)(2,1)} async-done(((bf16[16,32,512]{2,1,0:T(8,128)(2,1)}), bf16[16,128,512]{2,1,0:T(8,128)(2,1)}) %all-gather.12.cloned.1.call-update) | async-done | bytes 2097168 | tf_op jit(solution)/shard_map/all_gather | solution.py:45
  344.5 4.8 convolution_bitcast_fusion
  349.3 5.5 copy.24
  354.8 5.5 copy.25
  360.3 7.9 %broadcast_in_dim.45 = f32[32,32,32,128]{3,1,2,0:T(8,128)} broadcast(f32[]{:T(128)} %constant.20.clone.1), dimensions={} | broadcast | bytes 16777220 | tf_op jit(solution)/shard_map/broadcast_in_dim | solution.py:15
  368.2 35.3 %scatter_fusion = f32[32,32,32,128]{3,1,2,0:T(8,128)} fusion(f32[32,32,32,128]{3,1,2,0:T(8,128)} %broadcast_in_dim.45, s32[256]{0:T(256)S(1)} %reshape.132, f32[256,32,128]{2,1,0:T(8,128)} %bitcast.123), kind=kCustom, calls=%fused_computation.4 | custom fusion | flops 1048576 | bytes 12584960 | tf_op jit(solution)/shard_map/scatter-add | solution.py:49
  403.5 35.3 %scatter_fusion.1 = f32[32,32,32,128]{3,1,2,0:T(8,128)} fusion(f32[32,32,32,128]{3,1,2,0:T(8,128)} %scatter_fusion, s32[256]{0:T(256)S(1)} %reshape.138, f32[256,32,128]{2,1,0:T(8,128)} %bitcast.124), kind=kCustom, calls=%fused_computation.5 | custom fusion | flops 1048576 | bytes 12584960 | tf_op jit(solution)/shard_map/scatter-add | solution.py:49
  438.9 11.7 %copy_bitcast_fusion = f32[32,32,4096]{2,1,0:T(8,128)} fusion(f32[32,32,32,128]{3,1,2,0:T(8,128)} %scatter_fusion.1), kind=kLoop, calls=%fused_computation.6 | loop fusion | bytes 33554432 | tf_op jit(solution)/shard_map/reshape | solution.py:53
  450.6 115.0 %reduce-scatter.2.cloned.1.call-done = f32[32,32,512]{2,1,0:T(8,128)} async-done(((f32[32,32,4096]{2,1,0:T(8,128)}), f32[32,32,512]{2,1,0:T(8,128)}) %reduce-scatter.2.cloned.1.call-update) | async-done | bytes 2097168 | tf_op jit(solution)/shard_map/reduce_scatter | solution.py:52
  (26 shorter events, 0.2 us)
Async XLA Ops:
  6.5 3.9 copy-start.4
  6.5 61.3 %all-gather.8.cloned.1.call-start = ((), (), s32[]{:S(2)}) async-start(), calls=%async_computation.1 | async-start | bytes 9437184 | tf_op jit(solution)/shard_map/all_gather | solution.py:14
  7.3 107.8 %all-gather.16.cloned.1.call-start = ((), (), s32[]{:S(2)}) async-start(), calls=%async_computation.6 | async-start | bytes 2621440 | tf_op jit(solution)/shard_map/all_gather | solution.py:25
  9.6 151.5 %all-gather.14.cloned.1.call-start = ((), (), s32[]{:S(2)}) async-start(), calls=%async_computation.5 | async-start | bytes 2621440 | tf_op jit(solution)/shard_map/all_gather | solution.py:25
  10.4 240.8 %all-reduce.3.cloned.1.call-start = ((), (), s32[]{:S(2)}) async-start(), calls=%async_computation.7 | async-start | bytes 4194304 | tf_op jit(solution)/shard_map/psum | solution.py:32
  98.5 16.6 %copy-start = (bf16[1,16,32,512]{3,2,1,0:T(8,128)(2,1)S(1)}, bf16[1,16,32,512]{3,2,1,0:T(8,128)(2,1)}, u32[]{:S(2)}) copy-start(bf16[1,16,32,512]{3,2,1,0:T(8,128)(2,1)} %get-tuple-element.13) | copy-start | bytes 1572868
  115.1 46.1 %copy-start.1 = (bf16[1,16,32,512]{3,2,1,0:T(8,128)(2,1)S(1)}, bf16[1,16,32,512]{3,2,1,0:T(8,128)(2,1)}, u32[]{:S(2)}) copy-start(bf16[1,16,32,512]{3,2,1,0:T(8,128)(2,1)} %get-tuple-element.14) | copy-start | bytes 1572868
  161.2 5.0 copy-start.2
  166.0 0.8 copy-start.3
  166.1 132.5 %all-gather.10.cloned.1.call-start = ((), (), s32[]{:S(2)}) async-start(), calls=%async_computation.2 | async-start | bytes 2621440 | tf_op jit(solution)/shard_map/all_gather | solution.py:45
  253.7 90.8 %all-gather.12.cloned.1.call-start = ((), (), s32[]{:S(2)}) async-start(), calls=%async_computation.3 | async-start | bytes 2621440 | tf_op jit(solution)/shard_map/all_gather | solution.py:45
  257.0 308.6 %reduce-scatter.2.cloned.1.call-start = ((), (), s32[]{:S(2)}) async-start(), calls=%async_computation.4 | async-start | bytes 18874368 | tf_op jit(solution)/shard_map/reduce_scatter | solution.py:52
Sparse Core Ops, SparseCore 0:
  9.2 58.5 all-gather.7
  69.4 45.6 all-gather.15
  116.7 44.4 all-gather.13
  166.2 84.9 all-reduce.2
  253.9 44.6 all-gather.9
  300.0 44.4 all-gather.11
  450.7 114.8 reduce-scatter.1
where the time goes:
time: 574 us; the launch traced here: 572 us
  waiting for transfers between devices  383 us (67%)
  other arithmetic  76.9 us (13%)
  local copies, waits for them, and re-layouts  74.4 us (13%)
  matrix products  23.9 us (4%)
  between operations  13.7 us (2%)
    reduce_scatter x1, waiting for transfers between devices, body(): lax.psum_scatter(totals.reshape(nblocks, rows_mine, nbasis), 'grid', scat...  115 us
    psum x1, waiting for transfers between devices, body(): intersection = lax.psum(intersection_part, 'rows')  84.3 us
    all_gather x2, waiting for transfers between devices, body(): lax.all_gather(potential, 'rows', axis=1, tiled=True)  71.1 us
    scatter-add x2, other arithmetic, body(): totals.at[blocks[:, None], :, blocks[None, :], :]  70.6 us
    all_gather x1, waiting for transfers between devices, body(): stripe = lax.all_gather(density, 'grid', axis=2, tiled=True)  57.3 us
    all_gather x2, waiting for transfers between devices, body(): lax.all_gather(local_values, 'rows', axis=1, tiled=True)  53.9 us
    gather x2, local copies, waits for them, and re-layouts, body(): jnp.take(stripe, blocks, axis=0)  12.4 us
    reshape x1, local copies, waits for them, and re-layouts, body(): totals.reshape(nblocks, rows_mine, nbasis)  11.7 us
  transfers between devices with their start and end apart: 7, of which 7 were waited for; matrix products, arithmetic and copies ran while one was open for 11% of the time, Pallas kernels for 0%

commit v1 on v0

--- a/solution.py
+++ b/solution.py
@@ -2,6 +2,11 @@
 import jax.numpy as jnp
 from jax import lax
 from jax.sharding import PartitionSpec as P
+
+
+def remake_the_orders(my_data):
+    near = jnp.sum(lax.all_gather(my_data, axis_name="rows"), axis=0)
+    return near
 
 
 def body(density, basis_values, grid_points, grid_weights, screened_blocks):
@@ -29,7 +34,7 @@
         intersection_part = lax.dot_general(
             x_mine, fmat, (((0,), (0,)), ((), ())), preferred_element_type=jnp.float32
         )
-        intersection = lax.psum(intersection_part, "rows")
+        intersection = remake_the_orders(intersection_part)
         places = grid_points[batch_index]
         weights = grid_weights[batch_index]
         diffs = places[:, :, None] - places[:, None, :]

time: 574 us -> 644 us (1.12)
  waiting for transfers between devices: 383 us -> 435 us
  local copies, waits for them, and re-layouts: 74.4 us -> 85.3 us
  other arithmetic: 76.9 us -> 87.1 us
    all_gather x0 -> x2, waiting for transfers between devices: none -> 143 us  [remake_the_orders(): near = jnp.sum(lax.all_gather(my_data, axis_name='rows'), axis=0)]
    psum x1 -> x0, waiting for transfers between devices: 84.3 us -> none  [body(): intersection = lax.psum(intersection_part, 'rows')]
    all_gather x0 -> x2, local copies, waits for them, and re-layouts: none -> 12.1 us  [remake_the_orders(): near = jnp.sum(lax.all_gather(my_data, axis_name='rows'), axis=0)]
    reduce_sum x0 -> x2, other arithmetic: none -> 10.2 us  [remake_the_orders(): near = jnp.sum(lax.all_gather(my_data, axis_name='rows'), axis=0)]
    all_gather x2, waiting for transfers between devices: 71.1 us -> 62.9 us  [body(): lax.all_gather(potential, 'rows', axis=1, tiled=True)]
  transfers between devices with their start and end apart: 7 -> 8, of which waited for: 7 -> 8; matrix products, arithmetic and copies ran while one was open for 11% -> 14% of each run, Pallas kernels for 0% -> 0%
where the time goes in v1:
time: 644 us; the launch traced here: 642 us
  waiting for transfers between devices  435 us (68%)
  other arithmetic  87.1 us (14%)
  local copies, waits for them, and re-layouts  85.3 us (13%)
  matrix products  20.8 us (3%)
  between operations  13.7 us (2%)
    all_gather x2, waiting for transfers between devices, remake_the_orders(): near = jnp.sum(lax.all_gather(my_data, axis_name='rows'), axis=0)  143 us
    reduce_scatter x1, waiting for transfers between devices, body(): lax.psum_scatter(totals.reshape(nblocks, rows_mine, nbasis), 'grid', scat...  115 us
    scatter-add x2, other arithmetic, body(): totals.at[blocks[:, None], :, blocks[None, :], :]  70.7 us
    all_gather x2, waiting for transfers between devices, body(): lax.all_gather(potential, 'rows', axis=1, tiled=True)  62.9 us
    all_gather x1, waiting for transfers between devices, body(): stripe = lax.all_gather(density, 'grid', axis=2, tiled=True)  57.4 us
    all_gather x2, waiting for transfers between devices, body(): lax.all_gather(local_values, 'rows', axis=1, tiled=True)  55 us
  transfers between devices with their start and end apart: 8, of which 8 were waited for; matrix products, arithmetic and copies ran while one was open for 14% of the time, Pallas kernels for 0%

profile of v1, /device:TPU:0, one launch (start us, length us, event | category | flops | bytes accessed | tf_op | source)
XLA Modules:
  0.0 642.5 jit_solution(6307232178698835145)
XLA Ops:
  6.5 0.7 all-gather.12.cloned.1.call-update
  7.3 2.3 fusion.56
  9.7 0.7 all-gather.22.cloned.1.call-update
  10.4 57.4 %all-gather.12.cloned.1.call-done = bf16[32,32,4096]{2,1,0:T(8,128)(2,1)} async-done(((bf16[32,32,512]{2,1,0:T(8,128)(2,1)}), bf16[32,32,4096]{2,1,0:T(8,128)(2,1)}) %all-gather.12.cloned.1.call-update) | async-done | bytes 8388624 | tf_op jit(solution)/shard_map/all_gather | solution.py:19
  67.8 6.2 gather_fusion
  74.0 2.7 broadcast_select_fusion.1
  76.7 1.3 copy.30
  78.0 3.6 copy.19
  81.6 3.2 gather_fusion.1
  84.8 30.3 %all-gather.18.cloned.1.call-done = bf16[1,16,128,512]{3,2,1,0:T(8,128)(2,1)} async-done(((bf16[1,16,32,512]{3,2,1,0:T(8,128)(2,1)}), bf16[1,16,128,512]{3,2,1,0:T(8,128)(2,1)}) %all-gather.18.cloned.1.call-update) | async-done | bytes 2097168 | tf_op jit(solution)/shard_map/all_gather | solution.py:30
  115.1 4.2 convolution_bitcast_fusion.3
  119.4 6.3 gather_fusion.2
  125.7 2.6 broadcast_select_fusion
  128.4 1.3 copy.31
  129.6 3.6 copy.23
  133.2 3.2 gather_fusion.3
  136.4 24.7 %all-gather.22.cloned.1.call-done = bf16[1,16,128,512]{3,2,1,0:T(8,128)(2,1)} async-done(((bf16[1,16,32,512]{3,2,1,0:T(8,128)(2,1)}), bf16[1,16,128,512]{3,2,1,0:T(8,128)(2,1)}) %all-gather.22.cloned.1.call-update) | async-done | bytes 2097168 | tf_op jit(solution)/shard_map/all_gather | solution.py:30
  161.2 4.3 convolution_bitcast_fusion.2
  165.5 0.2 all-gather.14.cloned.1.call-start
  165.8 0.4 multiply_reduce_fusion.1
  166.2 0.3 copy.18
  166.5 75.6 %all-gather.20.cloned.1.call-done = f32[2048,512]{0,1:T(8,128)} async-done(((f32[512,512]{0,1:T(8,128)}), f32[2048,512]{0,1:T(8,128)}) %all-gather.20.cloned.1.call-update) | async-done | bytes 4194320 | tf_op jit(solution)/shard_map/all_gather | solution.py:8
  242.2 6.1 reshape.145
  248.2 5.2 reduce_sum.37
  253.4 1.3 fusion.20
  254.8 0.4 multiply_reduce_fusion
  255.2 0.3 copy.22
  255.5 67.3 %all-gather.24.cloned.1.call-done = f32[2048,512]{0,1:T(8,128)} async-done(((f32[512,512]{0,1:T(8,128)}), f32[2048,512]{0,1:T(8,128)}) %all-gather.24.cloned.1.call-update) | async-done | bytes 4194320 | tf_op jit(solution)/shard_map/all_gather | solution.py:8
  322.8 6.1 reshape.147
  328.9 5.0 reduce_sum.39
  333.9 1.3 fusion.21
  335.2 0.3 reduce-scatter.2.cloned.1.call-start
  335.6 0.1 or_select_fusion
  335.7 0.1 reshape.138
  335.7 0.1 reshape.132
  335.8 32.6 %all-gather.14.cloned.1.call-done = bf16[16,128,512]{2,1,0:T(8,128)(2,1)} async-done(((bf16[16,32,512]{2,1,0:T(8,128)(2,1)}), bf16[16,128,512]{2,1,0:T(8,128)(2,1)}) %all-gather.14.cloned.1.call-update) | async-done | bytes 2097168 | tf_op jit(solution)/shard_map/all_gather | solution.py:50
  368.4 4.8 convolution_bitcast_fusion.1
  373.3 5.5 copy.20
  378.8 5.4 copy.21
  384.2 30.3 %all-gather.16.cloned.1.call-done = bf16[16,128,512]{2,1,0:T(8,128)(2,1)} async-done(((bf16[16,32,512]{2,1,0:T(8,128)(2,1)}), bf16[16,128,512]{2,1,0:T(8,128)(2,1)}) %all-gather.16.cloned.1.call-update) | async-done | bytes 2097168 | tf_op jit(solution)/shard_map/all_gather | solution.py:50
  414.5 4.8 convolution_bitcast_fusion
  419.3 5.5 copy.24
  424.8 5.5 copy.25
  430.3 7.9 %broadcast_in_dim.45 = f32[32,32,32,128]{3,1,2,0:T(8,128)} broadcast(f32[]{:T(128)} %constant.20.clone.1), dimensions={} | broadcast | bytes 16777220 | tf_op jit(solution)/shard_map/broadcast_in_dim | solution.py:20
  438.2 35.3 %scatter_fusion = f32[32,32,32,128]{3,1,2,0:T(8,128)} fusion(f32[32,32,32,128]{3,1,2,0:T(8,128)} %broadcast_in_dim.45, s32[256]{0:T(256)S(1)} %reshape.132, f32[256,32,128]{2,1,0:T(8,128)} %bitcast.127), kind=kCustom, calls=%fused_computation.4 | custom fusion | flops 1048576 | bytes 12584960 | tf_op jit(solution)/shard_map/scatter-add | solution.py:54
  473.5 35.4 %scatter_fusion.1 = f32[32,32,32,128]{3,1,2,0:T(8,128)} fusion(f32[32,32,32,128]{3,1,2,0:T(8,128)} %scatter_fusion, s32[256]{0:T(256)S(1)} %reshape.138, f32[256,32,128]{2,1,0:T(8,128)} %bitcast.128), kind=kCustom, calls=%fused_computation.5 | custom fusion | flops 1048576 | bytes 12584960 | tf_op jit(solution)/shard_map/scatter-add | solution.py:54
  508.9 11.7 %copy_bitcast_fusion = f32[32,32,4096]{2,1,0:T(8,128)} fusion(f32[32,32,32,128]{3,1,2,0:T(8,128)} %scatter_fusion.1), kind=kLoop, calls=%fused_computation.6 | loop fusion | bytes 33554432 | tf_op jit(solution)/shard_map/reshape | solution.py:58
  520.6 115.1 %reduce-scatter.2.cloned.1.call-done = f32[32,32,512]{2,1,0:T(8,128)} async-done(((f32[32,32,4096]{2,1,0:T(8,128)}), f32[32,32,512]{2,1,0:T(8,128)}) %reduce-scatter.2.cloned.1.call-update) | async-done | bytes 2097168 | tf_op jit(solution)/shard_map/reduce_scatter | solution.py:57
  (33 shorter events, 0.4 us)
Async XLA Ops:
  6.5 3.9 copy-start.4
  6.5 61.3 %all-gather.12.cloned.1.call-start = ((), (), s32[]{:S(2)}) async-start(), calls=%async_computation.1 | async-start | bytes 9437184 | tf_op jit(solution)/shard_map/all_gather | solution.py:19
  7.3 107.8 %all-gather.18.cloned.1.call-start = ((), (), s32[]{:S(2)}) async-start(), calls=%async_computation.5 | async-start | bytes 2621440 | tf_op jit(solution)/shard_map/all_gather | solution.py:30
  9.6 151.6 %all-gather.22.cloned.1.call-start = ((), (), s32[]{:S(2)}) async-start(), calls=%async_computation.7 | async-start | bytes 2621440 | tf_op jit(solution)/shard_map/all_gather | solution.py:30
  10.3 231.8 %all-gather.20.cloned.1.call-start = ((), (), s32[]{:S(2)}) async-start(), calls=%async_computation.6 | async-start | bytes 5242880 | tf_op jit(solution)/shard_map/all_gather | solution.py:8
  81.6 33.5 %copy-start.1 = (bf16[1,16,32,512]{3,2,1,0:T(8,128)(2,1)S(1)}, bf16[1,16,32,512]{3,2,1,0:T(8,128)(2,1)}, u32[]{:S(2)}) copy-start(bf16[1,16,32,512]{3,2,1,0:T(8,128)(2,1)} %get-tuple-element.12) | copy-start | bytes 1572868
  119.4 203.5 %all-gather.24.cloned.1.call-start = ((), (), s32[]{:S(2)}) async-start(), calls=%async_computation.8 | async-start | bytes 5242880 | tf_op jit(solution)/shard_map/all_gather | solution.py:8
  133.2 27.9 %copy-start = (bf16[1,16,32,512]{3,2,1,0:T(8,128)(2,1)S(1)}, bf16[1,16,32,512]{3,2,1,0:T(8,128)(2,1)}, u32[]{:S(2)}) copy-start(bf16[1,16,32,512]{3,2,1,0:T(8,128)(2,1)} %get-tuple-element.11) | copy-start | bytes 1572868
  161.2 4.6 copy-start.2
  165.5 1.0 copy-start.3
  165.5 202.9 %all-gather.14.cloned.1.call-start = ((), (), s32[]{:S(2)}) async-start(), calls=%async_computation.2 | async-start | bytes 2621440 | tf_op jit(solution)/shard_map/all_gather | solution.py:50
  254.7 159.8 %all-gather.16.cloned.1.call-start = ((), (), s32[]{:S(2)}) async-start(), calls=%async_computation.3 | async-start | bytes 2621440 | tf_op jit(solution)/shard_map/all_gather | solution.py:50
  335.2 300.4 %reduce-scatter.2.cloned.1.call-start = ((), (), s32[]{:S(2)}) async-start(), calls=%async_computation.4 | async-start | bytes 18874368 | tf_op jit(solution)/shard_map/reduce_scatter | solution.py:57
Sparse Core Ops, SparseCore 0:
  9.2 58.5 all-gather.11
  69.4 45.6 all-gather.17
  116.7 44.4 all-gather.21
  162.6 79.5 all-gather.19
  243.6 79.2 all-gather.23
  324.3 44.1 all-gather.13
  370.0 44.4 all-gather.15
  520.7 114.9 reduce-scatter.1
